TPU v7x, 128 devices: a whole 4x4x4 slice. The times are simulated.
128 devices in a mesh: blk: 16 (over z, x_hi, core), head: 8 (over y, x_lo).
Axes of the slice: x: 4 (x_hi: 2, x_lo: 2; x = x_hi * 2 + x_lo), y: 4, z: 4, core: 2. Of those that a mesh axis runs over, the one named last changes fastest.
Arguments:
- queries: bfloat16 [4096, 8192], P('blk', 'head'), may hold values from -4 to 10
- context_keys: bfloat16 [16384, 1024], P('blk', 'head'), may hold values from -4 to 7
- context_values: bfloat16 [16384, 1024], P('blk', 'head'), may hold values from -6 to 6
- response_keys: bfloat16 [4096, 1024], P('blk', 'head'), may hold values from -4 to 7
- response_values: bfloat16 [4096, 1024], P('blk', 'head'), may hold values from -6 to 6
- out_weight: bfloat16 [8192, 8192], P('head', 'blk'), may hold values from -0.09375 to 0.09375
- query_docs: int32 [32], replicated, may hold values from 0 to 2
- block_docs: int32 [128], replicated, may hold values from 0 to 2
- visits: int32 [32, 4, 8], replicated, may hold values 0 or 1
Outputs:
- mixed: bfloat16 [4096, 8192], P('blk', 'head')
All inputs are finite; a program needn't handle non-finite values.
Results may differ from a plain program's by a relative error of at most 0.0165.
Values may be sent and summed in bfloat16 or wider, within the bound.
No kernel may reach another device: no remote copies, remote signals or barrier semaphores. Data moves between devices by JAX's collectives and lax.ppermute only.
A program may use at most 128 MiB of HBM per device.

v0:
```python
import jax
import jax.numpy as jnp
from jax import lax
from jax.sharding import PartitionSpec as P

HQ = 64
KVH = 8
HD = 128
BLOCK = 128
HOPS = 3


def from_behind(value, axis, by):
    devices = lax.axis_size(axis)
    return lax.ppermute(value, axis, [(i, (i + by) % devices) for i in range(devices)])


def attend(running, highest, weight_sum, query_heads, key_block, value_block, allowed):
    rows_here, heads_here, per_group, width = query_heads.shape
    key_heads = key_block.reshape(-1, heads_here, width)
    value_heads = value_block.reshape(-1, heads_here, width)
    scores = jnp.einsum(
        "tgjd,sgd->tgjs", query_heads, key_heads, preferred_element_type=jnp.float32
    ) * HD ** (-0.5)
    scores = jnp.where(allowed[:, None, None, :], scores, -jnp.inf)
    previous = highest.reshape(rows_here, heads_here, per_group)
    new_top = jnp.maximum(previous, jnp.max(scores, axis=-1))
    weights = jnp.exp(scores - new_top[..., None])
    factor = jnp.exp(previous - new_top)
    new_sum = weight_sum.reshape(rows_here, heads_here, per_group) * factor + jnp.sum(
        weights, axis=-1
    )
    partial_value = jnp.einsum(
        "tgjs,sgd->tgjd",
        weights.astype(jnp.bfloat16),
        value_heads,
        preferred_element_type=jnp.float32,
    )
    new_running = (
        running.reshape(rows_here, heads_here, per_group, width) * factor[..., None] + partial_value
    )
    return (
        new_running.reshape(rows_here, -1),
        new_top.reshape(rows_here, -1),
        new_sum.reshape(rows_here, -1),
    )


def block_allow(query_docs, block_docs, visits, anchor, holder, stride, rows_here, key_rows):
    blocks_q = rows_here // BLOCK
    blocks_k = key_rows // BLOCK
    query_doc = lax.dynamic_slice_in_dim(query_docs, anchor * blocks_q, blocks_q)
    block_doc = lax.dynamic_slice_in_dim(block_docs, holder * blocks_k, blocks_k)
    visited = lax.dynamic_slice_in_dim(visits, anchor * blocks_q, blocks_q)[:, stride, :]
    allowed = (visited == 1) & (query_doc[:, None] == block_doc[None, :])
    return jnp.repeat(jnp.repeat(allowed, BLOCK, axis=0), BLOCK, axis=1)


def shards(
    queries,
    context_keys,
    context_values,
    response_keys,
    response_values,
    out_weight,
    query_docs,
    block_docs,
    visits,
):
    rows_here = queries.shape[0]
    key_rows = context_keys.shape[0]
    heads_here = context_keys.shape[1] // HD
    per_group = HQ // KVH
    blk_count = lax.axis_size("blk")
    position = lax.axis_index("blk")
    query_heads = queries.reshape(rows_here, heads_here, per_group, HD)
    lanes = heads_here * per_group
    running = jnp.zeros((rows_here, lanes * HD), jnp.float32)
    highest = jnp.full((rows_here, lanes), -jnp.inf, jnp.float32)
    weight_sum = jnp.zeros((rows_here, lanes), jnp.float32)
    places = jnp.arange(rows_here)
    causal = places[:, None] >= places[None, :]
    running, highest, weight_sum = attend(
        running, highest, weight_sum, query_heads, response_keys, response_values, causal
    )
    key_block = context_keys
    value_block = context_values
    for stride in range(HOPS + 1):
        if stride > 0:
            key_block, value_block = from_behind((key_block, value_block), "blk", -1)
        holder = (position + stride) % blk_count
        allowed = block_allow(
            query_docs, block_docs, visits, position, holder, stride, rows_here, key_rows
        )
        running, highest, weight_sum = attend(
            running, highest, weight_sum, query_heads, key_block, value_block, allowed
        )
    attended = (
        (running.reshape(rows_here, lanes, HD) / weight_sum[:, :, None])
        .reshape(rows_here, -1)
        .astype(jnp.bfloat16)
    )
    products = jnp.dot(
        attended,
        lax.all_gather(out_weight, "blk", axis=1, tiled=True),
        preferred_element_type=jnp.float32,
    )
    mixed = lax.psum_scatter(products.astype(jnp.bfloat16), "head", scatter_dimension=1, tiled=True)
    return mixed


def solution(mesh):
    in_specs = (
        P("blk", "head"),
        P("blk", "head"),
        P("blk", "head"),
        P("blk", "head"),
        P("blk", "head"),
        P("head", "blk"),
        P(),
        P(),
        P(),
    )
    out_specs = P("blk", "head")
    return jax.shard_map(shards, mesh=mesh, in_specs=in_specs, out_specs=out_specs, check_vma=False)
```

profile of v0, /device:TPU:1, one launch (start us, length us, event | category | flops | bytes accessed | tf_op | source)
XLA Modules:
  0.0 247.4 jit_solution(1820500035767872004)
XLA Ops:
  6.5 0.7 all-gather.2.cloned.1.call-update
  7.3 1.5 collective-permute-start
  8.8 1.1 copy.19
  9.8 6.1 %collective-permute-start.1 = (bf16[1024,128]{0,1:T(8,128)(2,1)S(1)}, bf16[1024,128]{0,1:T(8,128)(2,1)S(1)}, u32[]{:S(2)}, u32[]{:S(2)}) collective-permute-start(bf16[1024,128]{0,1:T(8,128)(2,1)S(1)} %copy.19), channel_id=1, source_target_pairs={{0,120},{8,0},{16,8},{24,16},{32,24},{40,32},{48,40},{56,48},{64,5... | collective-permute-start | bytes 786440 | tf_op jit(solution)/shard_map/ppermute | solution.py:15
  16.0 0.8 dynamic-slice_compare_fusion.3
  16.8 0.1 copy.13
  16.9 0.1 copy.17
  17.1 0.1 copy.24
  17.2 0.7 dynamic_slice.25
  17.9 0.9 fusion.102
  19.0 1.3 fusion.103
  20.3 2.3 fusion.8
  22.6 0.3 fusion.28
  23.0 0.7 collective-permute-start.2
  23.7 0.7 collective-permute-start.3
  24.5 1.3 fusion.9
  25.9 10.3 %collective-permute-done.2 = bf16[1024,128]{1,0:T(8,128)(2,1)S(1)} collective-permute-done((bf16[1024,128]{1,0:T(8,128)(2,1)S(1)}, bf16[1024,128]{1,0:T(8,128)(2,1)S(1)}, u32[]{:S(2)}, u32[]{:S(2)}) %collective-permute-start.2) | collective-permute-done | bytes 262176 | tf_op jit(solution)/shard_map/ppermute | solution.py:15
  36.2 8.3 %collective-permute-done.3 = bf16[1024,128]{0,1:T(8,128)(2,1)S(1)} collective-permute-done((bf16[1024,128]{0,1:T(8,128)(2,1)S(1)}, bf16[1024,128]{0,1:T(8,128)(2,1)S(1)}, u32[]{:S(2)}, u32[]{:S(2)}) %collective-permute-start.3) | collective-permute-done | bytes 262176 | tf_op jit(solution)/shard_map/ppermute | solution.py:15
  44.6 4.6 %fusion.10 = (f32[256,8]{0,1:T(8,128)S(1)}, f32[1024,256,8]{1,0,2:T(8,128)}) fusion(pred[256,1024]{0,1:T(8,128)(4,1)S(1)} %bitcast.271, bf16[1024,128]{1,0:T(8,128)(2,1)S(1)} %collective-permute-done.2, bf16[256,1024]{1,0:T(8,128)(2,1)S(1)} %copy-done), kind=kOutput, calls=%fused_computation.19 | convolution fusion | flops 543160320 | bytes 9445376 | tf_op jit(solution)/shard_map/tgjd,sgd->tgjs/dot_general | solution.py:22
  49.3 1.3 fusion.11
  50.6 1.7 fusion
  52.3 1.7 fusion.2
  54.1 5.3 %fusion.4 = f32[256,8]{0,1:T(8,128)S(1)} fusion(f32[1024,256,8]{1,0,2:T(8,128)} %get-tuple-element.32, f32[256,8]{0,1:T(8,128)S(1)} %get-tuple-element.11, pred[256,1024]{0,1:T(8,128)(4,1)S(1)} %bitcast.272), kind=kLoop, calls=%fused_computation.13 | loop fusion | flops 8386560 | bytes 8667136 | tf_op jit(solution)/shard_map/reduce_sum | solution.py:30
  59.4 1.7 fusion.6
  61.2 0.5 fusion.64
  61.7 2.4 fusion.60
  64.1 2.3 fusion.57
  66.5 2.3 fusion.54
  68.8 2.3 fusion.51
  71.2 69.6 %all-gather.2.cloned.1.call-done = bf16[1024,8192]{1,0:T(8,128)(2,1)} async-done(((bf16[1024,512]{1,0:T(8,128)(2,1)}), bf16[1024,8192]{1,0:T(8,128)(2,1)}) %all-gather.2.cloned.1.call-update) | async-done | bytes 16777232 | tf_op jit(solution)/shard_map/all_gather | solution.py:105
  140.8 12.0 %convolution_convert_fusion = bf16[256,8192]{1,0:T(8,128)(2,1)} fusion(bf16[256,1024]{0,1:T(8,128)(2,1)S(1)} %fusion.67, bf16[1024,8192]{1,0:T(8,128)(2,1)} %all-gather.2.cloned.1.call-done), kind=kOutput, calls=%fused_computation | convolution fusion | flops 4297064448 | bytes 21495808 | tf_op jit(solution)/shard_map/dot_general | solution.py:103
  152.8 87.7 %reduce-scatter.2.cloned.1.call-done = bf16[256,1024]{1,0:T(8,128)(2,1)} async-done(((bf16[256,8192]{1,0:T(8,128)(2,1)}), bf16[256,1024]{1,0:T(8,128)(2,1)}) %reduce-scatter.2.cloned.1.call-update) | async-done | bytes 524304 | tf_op jit(solution)/shard_map/reduce_scatter | solution.py:108
  (34 shorter events, 0.9 us)
Async XLA Ops:
  6.5 12.4 %copy-start = (bf16[256,1024]{1,0:T(8,128)(2,1)S(1)}, bf16[256,1024]{1,0:T(8,128)(2,1)}, u32[]{:S(2)}) copy-start(bf16[256,1024]{1,0:T(8,128)(2,1)} %param.9) | copy-start | bytes 1572868
  6.5 134.2 %all-gather.2.cloned.1.call-start = ((), (), s32[]{:S(2)}) async-start(), calls=%async_computation.1 | async-start | bytes 17825792 | tf_op jit(solution)/shard_map/all_gather | solution.py:105
  7.3 233.3 %reduce-scatter.2.cloned.1.call-start = ((), (), s32[]{:S(2)}) async-start(), calls=%async_computation.2 | async-start | bytes 4718592 | tf_op jit(solution)/shard_map/reduce_scatter | solution.py:108
  7.3 15.7 %collective-permute-start = (bf16[1024,128]{1,0:T(8,128)(2,1)}, bf16[1024,128]{1,0:T(8,128)(2,1)S(1)}, u32[]{:S(2)}, u32[]{:S(2)}) collective-permute-start(bf16[1024,128]{1,0:T(8,128)(2,1)} %param.10), channel_id=1, source_target_pairs={{0,120},{8,0},{16,8},{24,16},{32,24},{40,32},{48,40},{56,48},{64,5... | collective-permute-start | bytes 786440 | tf_op jit(solution)/shard_map/ppermute | solution.py:15
  9.8 13.9 %collective-permute-start.1 = (bf16[1024,128]{0,1:T(8,128)(2,1)S(1)}, bf16[1024,128]{0,1:T(8,128)(2,1)S(1)}, u32[]{:S(2)}, u32[]{:S(2)}) collective-permute-start(bf16[1024,128]{0,1:T(8,128)(2,1)S(1)} %copy.19), channel_id=1, source_target_pairs={{0,120},{8,0},{16,8},{24,16},{32,24},{40,32},{48,40},{56,48},{64,5... | collective-permute-start | bytes 786440 | tf_op jit(solution)/shard_map/ppermute | solution.py:15
  23.0 13.2 %collective-permute-start.2 = (bf16[1024,128]{1,0:T(8,128)(2,1)S(1)}, bf16[1024,128]{1,0:T(8,128)(2,1)S(1)}, u32[]{:S(2)}, u32[]{:S(2)}) collective-permute-start(bf16[1024,128]{1,0:T(8,128)(2,1)S(1)} %collective-permute-done), channel_id=1, source_target_pairs={{0,120},{8,0},{16,8},{24,16},{32,24},{40,32},{48,40},{56,48},{64,5... | collective-permute-start | bytes 786440 | tf_op jit(solution)/shard_map/ppermute | solution.py:15
  23.7 20.8 %collective-permute-start.3 = (bf16[1024,128]{0,1:T(8,128)(2,1)S(1)}, bf16[1024,128]{0,1:T(8,128)(2,1)S(1)}, u32[]{:S(2)}, u32[]{:S(2)}) collective-permute-start(bf16[1024,128]{0,1:T(8,128)(2,1)S(1)} %collective-permute-done.1), channel_id=1, source_target_pairs={{0,120},{8,0},{16,8},{24,16},{32,24},{40,32},{48,40},{56,48},{64,5... | collective-permute-start | bytes 786440 | tf_op jit(solution)/shard_map/ppermute | solution.py:15
  36.2 13.0 %collective-permute-start.4 = (bf16[1024,128]{1,0:T(8,128)(2,1)S(1)}, bf16[1024,128]{1,0:T(8,128)(2,1)S(1)}, u32[]{:S(2)}, u32[]{:S(2)}) collective-permute-start(bf16[1024,128]{1,0:T(8,128)(2,1)S(1)} %collective-permute-done.2), channel_id=1, source_target_pairs={{0,120},{8,0},{16,8},{24,16},{32,24},{40,32},{48,40},{56,48},{64,5... | collective-permute-start | bytes 786440 | tf_op jit(solution)/shard_map/ppermute | solution.py:15
  44.5 24.3 %collective-permute-start.5 = (bf16[1024,128]{0,1:T(8,128)(2,1)S(1)}, bf16[1024,128]{0,1:T(8,128)(2,1)S(1)}, u32[]{:S(2)}, u32[]{:S(2)}) collective-permute-start(bf16[1024,128]{0,1:T(8,128)(2,1)S(1)} %collective-permute-done.3), channel_id=1, source_target_pairs={{0,120},{8,0},{16,8},{24,16},{32,24},{40,32},{48,40},{56,48},{64,5... | collective-permute-start | bytes 786440 | tf_op jit(solution)/shard_map/ppermute | solution.py:15
  54.0 7.1 %copy-start.3 = (bf16[256,128]{1,0:T(8,128)(2,1)S(1)}, bf16[256,128]{1,0:T(8,128)(2,1)}, u32[]{:S(2)}) copy-start(bf16[256,128]{1,0:T(8,128)(2,1)} %param.13) | copy-start | bytes 196612
  54.1 7.6 %copy-start.2 = (bf16[1024,128]{1,0:T(8,128)(2,1)S(1)}, bf16[1024,128]{1,0:T(8,128)(2,1)}, u32[]{:S(2)}) copy-start(bf16[1024,128]{1,0:T(8,128)(2,1)} %param.11) | copy-start | bytes 786436
  61.2 5.3 %slice-start = ((s8[8388608]{0:T(1024)(128)(4,1)}), s8[4194304]{0:T(1024)(128)(4,1)S(1)}, s32[]{:S(2)}) async-start(s8[8388608]{0:T(1024)(128)(4,1)} %bitcast.260), calls=%async_computation.3 | async-start | bytes 8388608
  61.7 4.8 %slice-start.1 = ((s8[8388608]{0:T(1024)(128)(4,1)}), s8[4194304]{0:T(1024)(128)(4,1)S(1)}, s32[]{:S(2)}) async-start(s8[8388608]{0:T(1024)(128)(4,1)} %bitcast.260), calls=%async_computation.4 | async-start | bytes 8388608
  71.1 169.5 %copy-start.1 = (bf16[256,1024]{1,0:T(8,128)(2,1)S(1)}, bf16[256,1024]{1,0:T(8,128)(2,1)}, u32[]{:S(2)}) copy-start(bf16[256,1024]{1,0:T(8,128)(2,1)} %param.9) | copy-start | bytes 1572868
Sparse Core Ops, SparseCore 0:
  9.7 131.0 all-gather.1
  153.0 87.5 reduce-scatter.1
where the time goes:
time: 248 us; the launch traced here: 247 us
  waiting for transfers between devices  177 us (71%)
  matrix products  32.7 us (13%)
  between operations  13.7 us (6%)
  other arithmetic  11.8 us (5%)
  starting transfers between devices  9.01 us (4%)
  local copies, waits for them, and re-layouts  3.55 us (1%)
    reduce_scatter x1, waiting for transfers between devices, shards(): lax.psum_scatter(products.astype(jnp.bfloat16), 'head', scatter_dimension...  87.7 us
    all_gather x1, waiting for transfers between devices, shards(): lax.all_gather(out_weight, 'blk', axis=1, tiled=True)  69.6 us
    ppermute x6, waiting for transfers between devices, from_behind(): lax.ppermute(value, axis, [(i, (i + by) % devices) for i in range(devices)])  18.7 us
    dot_general x1, matrix products, shards(): jnp.dot(attended, lax.all_gather(out_weight, 'blk', axis=1, tiled=True),...  12 us
    dot_general x5, matrix products, attend(): jnp.einsum('tgjd,sgd->tgjs', query_heads, key_heads, preferred_element_ty...  10.8 us
    reduce_sum x5, other arithmetic, attend(): jnp.sum(weights, axis=-1)  10.7 us
    dot_general x5, matrix products, attend(): jnp.einsum('tgjs,sgd->tgjd', weights.astype(jnp.bfloat16), value_heads, p...  9.86 us
    ppermute x6, starting transfers between devices, from_behind(): lax.ppermute(value, axis, [(i, (i + by) % devices) for i in range(devices)])  8.97 us
  transfers between devices with their start and end apart: 8, of which 4 were waited for; matrix products, arithmetic and copies ran while one was open for 15% of the time, Pallas kernels for 0%

commit v1 on v0

--- a/solution.py
+++ b/solution.py
@@ -102,7 +102,9 @@
     )
     products = jnp.dot(
         attended,
-        lax.all_gather(out_weight, "blk", axis=1, tiled=True),
+        jnp.concatenate(
+            lax.all_to_all(jnp.stack([out_weight] * lax.axis_size("blk")), "blk", 0, 0), axis=1
+        ),
         preferred_element_type=jnp.float32,
     )
     mixed = lax.psum_scatter(products.astype(jnp.bfloat16), "head", scatter_dimension=1, tiled=True)

time: 248 us -> 358 us (1.44)
  waiting for transfers between devices: 177 us -> 279 us
  starting transfers between devices: 9.01 us -> 17.3 us
  local copies, waits for them, and re-layouts: 3.55 us -> 8.7 us
  matrix products: 32.7 us -> 28.6 us
    ppermute x6, waiting for transfers between devices: 18.7 us -> 187 us  [from_behind(): lax.ppermute(value, axis, [(i, (i + by) % devices) for i in range(devices)])]
    all_gather x1 -> x0, waiting for transfers between devices: 69.6 us -> none  [shards(): lax.all_gather(out_weight, 'blk', axis=1, tiled=True)]
    all_to_all x0 -> x1, starting transfers between devices: none -> 9.42 us  [shards(): lax.all_to_all(jnp.stack([out_weight] * lax.axis_size('blk')), 'blk', 0, 0)]
    another operation x0 -> x1, local copies, waits for them, and re-layouts: none -> 5.98 us  [shards(): jnp.stack([out_weight] * lax.axis_size('blk'))]
  transfers between devices with their start and end apart: 8 -> 8, of which waited for: 4 -> 5; matrix products, arithmetic and copies ran while one was open for 15% -> 9% of each run, Pallas kernels for 0% -> 0%
where the time goes in v1:
time: 358 us
  waiting for transfers between devices  279 us (78%)
  matrix products  28.6 us (8%)
  starting transfers between devices  17.3 us (5%)
  between operations  13.7 us (4%)
  other arithmetic  10.8 us (3%)
  local copies, waits for them, and re-layouts  8.7 us (2%)
    ppermute x6, waiting for transfers between devices, from_behind(): lax.ppermute(value, axis, [(i, (i + by) % devices) for i in range(devices)])  187 us
    reduce_scatter x1, waiting for transfers between devices, shards(): lax.psum_scatter(products.astype(jnp.bfloat16), 'head', scatter_dimension...  91.1 us
    reduce_sum x5, other arithmetic, attend(): jnp.sum(weights, axis=-1)  10.6 us
    dot_general x5, matrix products, attend(): jnp.einsum('tgjs,sgd->tgjd', weights.astype(jnp.bfloat16), value_heads, p...  9.88 us
    dot_general x1, matrix products, shards(): jnp.dot(attended, jnp.concatenate(lax.all_to_all(jnp.stack([out_weight] *...  9.64 us
    all_to_all x1, starting transfers between devices, shards(): lax.all_to_all(jnp.stack([out_weight] * lax.axis_size('blk')), 'blk', 0, 0)  9.42 us
    dot_general x5, matrix products, attend(): jnp.einsum('tgjd,sgd->tgjs', query_heads, key_heads, preferred_element_ty...  9.06 us
    ppermute x6, starting transfers between devices, from_behind(): lax.ppermute(value, axis, [(i, (i + by) % devices) for i in range(devices)])  7.81 us
  transfers between devices with their start and end apart: 8, of which 5 were waited for; matrix products, arithmetic and copies ran while one was open for 9% of the time, Pallas kernels for 0%

profile of v1, /device:TPU:1, one launch (start us, length us, event | category | flops | bytes accessed | tf_op | source)
XLA Modules:
  0.0 357.6 jit_solution(16802652298314236321)
XLA Ops:
  6.5 1.5 copy.44
  8.1 6.0 %stack.2 = bf16[16,1024,512]{1,2,0:T(8,128)(2,1)} broadcast(bf16[1024,512]{0,1:T(8,128)(2,1)S(1)} %copy.44), dimensions={1,2} | broadcast | bytes 17825792 | tf_op jit(solution)/shard_map/stack | solution.py:106
  14.1 9.4 %all-to-all-start = ((bf16[16,1024,512]{1,2,0:T(8,128)(2,1)}), bf16[16,1024,512]{1,2,0:T(8,128)(2,1)}, u32[]{:S(2)}, u32[]{:S(2)}) async-start(bf16[16,1024,512]{1,2,0:T(8,128)(2,1)} %stack.2), calls=%async_computation | async-start | bytes 33554432 | tf_op jit(solution)/shard_map/all_to_all | solution.py:106
  23.6 0.2 collective-permute-start
  23.8 0.1 copy.36
  24.0 5.3 %collective-permute-start.1 = (bf16[1024,128]{0,1:T(8,128)(2,1)S(1)}, bf16[1024,128]{0,1:T(8,128)(2,1)S(1)}, u32[]{:S(2)}, u32[]{:S(2)}) collective-permute-start(bf16[1024,128]{0,1:T(8,128)(2,1)S(1)} %copy.36), channel_id=1, source_target_pairs={{0,120},{8,0},{16,8},{24,16},{32,24},{40,32},{48,40},{56,48},{64,5... | collective-permute-start | bytes 786440 | tf_op jit(solution)/shard_map/ppermute | solution.py:15
  29.3 0.1 copy.30
  29.4 0.1 copy.34
  29.5 0.1 copy.38
  29.6 0.1 copy.41
  30.1 0.5 fusion.104
  30.6 1.3 fusion.8
  32.0 0.3 fusion.28
  32.3 178.9 %collective-permute-done = bf16[1024,128]{1,0:T(8,128)(2,1)S(1)} collective-permute-done((bf16[1024,128]{1,0:T(8,128)(2,1)S(1)}, bf16[1024,128]{1,0:T(8,128)(2,1)S(1)}, u32[]{:S(2)}, u32[]{:S(2)}) %collective-permute-start) | collective-permute-done | bytes 262176 | tf_op jit(solution)/shard_map/ppermute | solution.py:15
  211.2 2.8 collective-permute-done.1
  214.2 1.3 fusion.9
  215.5 3.0 collective-permute-done.2
  218.5 2.8 collective-permute-done.3
  221.3 2.2 collective-permute-start.5
  223.6 4.6 %fusion.10 = (f32[256,8]{0,1:T(8,128)S(1)}, f32[1024,256,8]{1,0,2:T(8,128)}) fusion(pred[256,1024]{0,1:T(8,128)(4,1)S(1)} %bitcast.275, bf16[1024,128]{1,0:T(8,128)(2,1)S(1)} %collective-permute-done.2, bf16[256,1024]{1,0:T(8,128)(2,1)S(1)} %copy-done), kind=kOutput, calls=%fused_computation.19 | convolution fusion | flops 543160320 | bytes 9445376 | tf_op jit(solution)/shard_map/tgjd,sgd->tgjs/dot_general | solution.py:22
  228.2 1.3 fusion.11
  229.6 1.7 fusion
  231.3 1.7 fusion.2
  233.0 5.2 %fusion.4 = f32[256,8]{0,1:T(8,128)S(1)} fusion(f32[1024,256,8]{1,0,2:T(8,128)} %get-tuple-element.32, f32[256,8]{0,1:T(8,128)S(1)} %get-tuple-element.11, pred[256,1024]{0,1:T(8,128)(4,1)S(1)} %bitcast.276), kind=kLoop, calls=%fused_computation.13 | loop fusion | flops 8386560 | bytes 8667136 | tf_op jit(solution)/shard_map/reduce_sum | solution.py:30
  238.2 1.7 fusion.6
  240.0 0.5 fusion.64
  240.5 2.4 fusion.60
  242.9 2.3 fusion.57
  245.3 2.3 fusion.54
  247.6 2.3 divide_convert_fusion
  250.0 9.6 %convolution_convert_fusion = bf16[256,8192]{1,0:T(8,128)(2,1)} fusion(bf16[256,1024]{0,1:T(8,128)(2,1)S(1)} %bitcast.278, bf16[1024,8192]{0,1:T(8,128)(2,1)} %bitcast.50), kind=kOutput, calls=%fused_computation | convolution fusion | flops 4297064448 | bytes 21495808 | tf_op jit(solution)/shard_map/dot_general | solution.py:103
  259.6 91.1 %reduce-scatter.2.cloned.1.call-done = bf16[256,1024]{1,0:T(8,128)(2,1)} async-done(((bf16[256,8192]{1,0:T(8,128)(2,1)}), bf16[256,1024]{1,0:T(8,128)(2,1)}) %reduce-scatter.2.cloned.1.call-update) | async-done | bytes 524304 | tf_op jit(solution)/shard_map/reduce_scatter | solution.py:110
  (44 shorter events, 1.0 us)
Async XLA Ops:
  6.5 23.5 %copy-start = (bf16[256,1024]{1,0:T(8,128)(2,1)S(1)}, bf16[256,1024]{1,0:T(8,128)(2,1)}, u32[]{:S(2)}) copy-start(bf16[256,1024]{1,0:T(8,128)(2,1)} %param.9) | copy-start | bytes 1572868
  14.1 9.5 %copy-start.2 = (bf16[1024,128]{1,0:T(8,128)(2,1)S(1)}, bf16[1024,128]{1,0:T(8,128)(2,1)}, u32[]{:S(2)}) copy-start(bf16[1024,128]{1,0:T(8,128)(2,1)} %param.10) | copy-start | bytes 786436
  14.1 9.7 %copy-start.3 = (bf16[1024,128]{1,0:T(8,128)(2,1)S(1)}, bf16[1024,128]{1,0:T(8,128)(2,1)}, u32[]{:S(2)}) copy-start(bf16[1024,128]{1,0:T(8,128)(2,1)} %param.11) | copy-start | bytes 786436
  14.1 15.2 %copy-start.6 = (s32[32,4,8]{0,2,1:T(8,128)S(1)}, s32[32,4,8]{0,2,1:T(8,128)}, u32[]{:S(2)}) copy-start(s32[32,4,8]{0,2,1:T(8,128)} %param.17) | copy-start | bytes 12292
  14.1 15.6 %copy-start.8 = (s32[32]{0:T(128)S(1)}, s32[32]{0:T(128)}, u32[]{:S(2)}) copy-start(s32[32]{0:T(128)} %param.15) | copy-start | bytes 388
  14.1 15.7 %copy-start.7 = (s32[128]{0:T(128)S(1)}, s32[128]{0:T(128)}, u32[]{:S(2)}) copy-start(s32[128]{0:T(128)} %param.16) | copy-start | bytes 1540
  14.1 16.0 %copy-start.4 = (bf16[256,128]{1,0:T(8,128)(2,1)S(1)}, bf16[256,128]{1,0:T(8,128)(2,1)}, u32[]{:S(2)}) copy-start(bf16[256,128]{1,0:T(8,128)(2,1)} %param.12) | copy-start | bytes 196612
  14.1 235.8 %all-to-all-start = ((bf16[16,1024,512]{1,2,0:T(8,128)(2,1)}), bf16[16,1024,512]{1,2,0:T(8,128)(2,1)}, u32[]{:S(2)}, u32[]{:S(2)}) async-start(bf16[16,1024,512]{1,2,0:T(8,128)(2,1)} %stack.2), calls=%async_computation | async-start | bytes 33554432 | tf_op jit(solution)/shard_map/all_to_all | solution.py:106
  23.5 327.2 %reduce-scatter.2.cloned.1.call-start = ((), (), s32[]{:S(2)}) async-start(), calls=%async_computation.2 | async-start | bytes 4718592 | tf_op jit(solution)/shard_map/reduce_scatter | solution.py:110
  23.6 187.6 %collective-permute-start = (bf16[1024,128]{1,0:T(8,128)(2,1)S(1)}, bf16[1024,128]{1,0:T(8,128)(2,1)S(1)}, u32[]{:S(2)}, u32[]{:S(2)}) collective-permute-start(bf16[1024,128]{1,0:T(8,128)(2,1)S(1)} %copy-done.2), channel_id=1, source_target_pairs={{0,120},{8,0},{16,8},{24,16},{32,24},{40,32},{48,40},{56,48},{64,5... | collective-permute-start | bytes 786440 | tf_op jit(solution)/shard_map/ppermute | solution.py:15
  24.0 190.1 %collective-permute-start.1 = (bf16[1024,128]{0,1:T(8,128)(2,1)S(1)}, bf16[1024,128]{0,1:T(8,128)(2,1)S(1)}, u32[]{:S(2)}, u32[]{:S(2)}) collective-permute-start(bf16[1024,128]{0,1:T(8,128)(2,1)S(1)} %copy.36), channel_id=1, source_target_pairs={{0,120},{8,0},{16,8},{24,16},{32,24},{40,32},{48,40},{56,48},{64,5... | collective-permute-start | bytes 786440 | tf_op jit(solution)/shard_map/ppermute | solution.py:15
  211.2 7.3 %collective-permute-start.2 = (bf16[1024,128]{1,0:T(8,128)(2,1)S(1)}, bf16[1024,128]{1,0:T(8,128)(2,1)S(1)}, u32[]{:S(2)}, u32[]{:S(2)}) collective-permute-start(bf16[1024,128]{1,0:T(8,128)(2,1)S(1)} %collective-permute-done), channel_id=1, source_target_pairs={{0,120},{8,0},{16,8},{24,16},{32,24},{40,32},{48,40},{56,48},{64,5... | collective-permute-start | bytes 786440 | tf_op jit(solution)/shard_map/ppermute | solution.py:15
  214.0 7.3 %collective-permute-start.3 = (bf16[1024,128]{0,1:T(8,128)(2,1)S(1)}, bf16[1024,128]{0,1:T(8,128)(2,1)S(1)}, u32[]{:S(2)}, u32[]{:S(2)}) collective-permute-start(bf16[1024,128]{0,1:T(8,128)(2,1)S(1)} %collective-permute-done.1), channel_id=1, source_target_pairs={{0,120},{8,0},{16,8},{24,16},{32,24},{40,32},{48,40},{56,48},{64,5... | collective-permute-start | bytes 786440 | tf_op jit(solution)/shard_map/ppermute | solution.py:15
  218.5 9.6 %collective-permute-start.4 = (bf16[1024,128]{1,0:T(8,128)(2,1)S(1)}, bf16[1024,128]{1,0:T(8,128)(2,1)S(1)}, u32[]{:S(2)}, u32[]{:S(2)}) collective-permute-start(bf16[1024,128]{1,0:T(8,128)(2,1)S(1)} %collective-permute-done.2), channel_id=1, source_target_pairs={{0,120},{8,0},{16,8},{24,16},{32,24},{40,32},{48,40},{56,48},{64,5... | collective-permute-start | bytes 786440 | tf_op jit(solution)/shard_map/ppermute | solution.py:15
  221.3 26.3 %collective-permute-start.5 = (bf16[1024,128]{0,1:T(8,128)(2,1)S(1)}, bf16[1024,128]{0,1:T(8,128)(2,1)S(1)}, u32[]{:S(2)}, u32[]{:S(2)}) collective-permute-start(bf16[1024,128]{0,1:T(8,128)(2,1)S(1)} %collective-permute-done.3), channel_id=1, source_target_pairs={{0,120},{8,0},{16,8},{24,16},{32,24},{40,32},{48,40},{56,48},{64,5... | collective-permute-start | bytes 786440 | tf_op jit(solution)/shard_map/ppermute | solution.py:15
  233.0 6.9 %copy-start.5 = (bf16[256,128]{1,0:T(8,128)(2,1)S(1)}, bf16[256,128]{1,0:T(8,128)(2,1)}, u32[]{:S(2)}) copy-start(bf16[256,128]{1,0:T(8,128)(2,1)} %param.13) | copy-start | bytes 196612
  240.0 5.3 %slice-start = ((s8[8388608]{0:T(1024)(128)(4,1)}), s8[4194304]{0:T(1024)(128)(4,1)S(1)}, s32[]{:S(2)}) async-start(s8[8388608]{0:T(1024)(128)(4,1)} %bitcast.264), calls=%async_computation.3 | async-start | bytes 8388608
  240.5 4.8 %slice-start.1 = ((s8[8388608]{0:T(1024)(128)(4,1)}), s8[4194304]{0:T(1024)(128)(4,1)S(1)}, s32[]{:S(2)}) async-start(s8[8388608]{0:T(1024)(128)(4,1)} %bitcast.264), calls=%async_computation.4 | async-start | bytes 8388608
  249.9 100.8 %copy-start.1 = (bf16[256,1024]{1,0:T(8,128)(2,1)S(1)}, bf16[256,1024]{1,0:T(8,128)(2,1)}, u32[]{:S(2)}) copy-start(bf16[256,1024]{1,0:T(8,128)(2,1)} %param.9) | copy-start | bytes 1572868
Sparse Core Ops, SparseCore 0:
  259.7 90.9 reduce-scatter.1
